TPU v7x, 32 devices: a whole 2x2x4 slice. The times are simulated.
32 devices in a mesh: batch: 8 (over y, x, core), head: 4 (over z).
Axes of the slice: x: 2, y: 2, z: 4, core: 2. Of those that a mesh axis runs over, the one named last changes fastest.
Arguments:
- inputs: bfloat16 [8, 128, 2048], P(None, 'batch', 'head'), parts along dimension 1, may hold values from -6 to 6
- in_weight: bfloat16 [2048, 4, 384], P(None, 'head'), may hold values from -0.125 to 0.125
- gate_weight: bfloat16 [2048, 4], P(None, 'head'), may hold values from -0.125 to 0.125
- gate_bias: float32 [4], P('head'), may hold values from -2 to 3
- norm_gain: float32 [512], P('head'), may hold values from 0.1 to 1.9
- out_weight: bfloat16 [512, 2048], P('head'), may hold values from -0.375 to 0.375
- inv_gram: float32 [128, 4, 128, 128], P('batch', 'head'), parts along dimension 0, may hold values from -17 to 17, as said below
- value_key: float32 [128, 4, 128, 128], P('batch', 'head'), parts along dimension 0, may hold values from -6 to 6
Outputs:
- layer_out: float32 [8, 128, 2048], P(None, 'batch', 'head'), parts along dimension 1
There are 8 independent parts, one for each index of `batch`. A program takes and returns all parts, laid end to end along the dimension named above; an argument that names none is the same for every part. Nothing has to cross between parts.
Inputs may be any that keep to these rules, and one draw needn't show every extreme that they name: `inv_gram`: each [128, 128] matrix is symmetric positive definite.
All inputs are finite; a program needn't handle non-finite values.
Results may differ from a plain program's by a relative error of at most 0.0029.
Values may be sent and summed in bfloat16 or wider, within the bound.
A program may use at most 64 MiB of HBM per device.

v0:
```python
import functools
import math

import jax
import jax.numpy as jnp
from jax import lax
from jax.experimental import pallas as pl
from jax.experimental.pallas import tpu as pltpu
from jax.sharding import PartitionSpec as P

MESH = pl.DeviceIdType.MESH
F32 = jnp.float32
BF16 = jnp.bfloat16
NT = (((1,), (1,)), ((), ()))


def split(x):
    hi = x.astype(BF16)
    lo = (x - hi.astype(F32)).astype(BF16)
    return hi, lo


def rowsum(x):
    return jnp.sum(x, axis=-1, keepdims=True)


def kernel(
    n,
    group,
    x_hbm,
    w_hbm,
    gate_hbm,
    bias_ref,
    gain_ref,
    ow_hbm,
    a_hbm,
    m_hbm,
    out_ref,
    xg,
    w,
    gate,
    a32,
    m32,
    a2,
    m2,
    wout,
    pacc,
    gacc,
    kbuf,
    qbuf,
    akbuf,
    aqbuf,
    wbuf,
    robuf,
    rbuf,
    sqbuf,
    lsem,
    xs,
    xr,
    w1s,
    w1r,
    w2s,
    w2r,
    rs,
    rr,
    qs,
    qr,
):
    steps, seqs, feats = x_hbm.shape
    rows = steps * seqs
    heads_rows = ow_hbm.shape[0]
    cols = ow_hbm.shape[1] // n
    size = a_hbm.shape[1]
    me = lax.axis_index("head")
    b = lax.axis_index("batch")
    mine = lax.rem(b, group)
    base = b - mine
    slab = heads_rows // group

    loads = [
        pltpu.make_async_copy(x_hbm, xg.at[me], lsem.at[0]),
        pltpu.make_async_copy(w_hbm, w, lsem.at[1]),
        pltpu.make_async_copy(gate_hbm, gate, lsem.at[2]),
        pltpu.make_async_copy(a_hbm, a32, lsem.at[3]),
        pltpu.make_async_copy(m_hbm, m32, lsem.at[4]),
        pltpu.make_async_copy(
            ow_hbm.at[:, pl.ds(pl.multiple_of(me * cols, cols), cols)], wout.at[me], lsem.at[5]
        ),
    ]
    for load in loads:
        load.start()

    barrier = pltpu.get_barrier_semaphore()

    for o in range(1, n):
        pl.semaphore_signal(
            barrier, inc=1, device_id={"head": lax.rem(me + o, n)}, device_id_type=MESH
        )
    for o in range(1, group):
        peer = base + lax.rem(mine + o, group)
        pl.semaphore_signal(barrier, inc=1, device_id={"batch": peer}, device_id_type=MESH)
    pl.semaphore_wait(barrier, n + group - 2)

    order = sorted(range(1, n), key=lambda o: -min(o, n - o))

    def xcopy(o):
        return pltpu.make_async_remote_copy(
            src_ref=xg.at[me],
            dst_ref=xg.at[me],
            send_sem=xs.at[o],
            recv_sem=xr.at[o],
            device_id={"head": lax.rem(me + o, n)},
            device_id_type=MESH,
        )

    loads[0].wait()
    for o in order:
        xcopy(o).start()

    def w1copy(o):
        other = lax.rem(me + o, n)
        return pltpu.make_async_remote_copy(
            src_ref=ow_hbm.at[
                pl.ds(pl.multiple_of(mine * slab, slab), slab),
                pl.ds(pl.multiple_of(other * cols, cols), cols),
            ],
            dst_ref=wout.at[me, pl.ds(pl.multiple_of(mine * slab, slab), slab)],
            send_sem=w1s.at[o],
            recv_sem=w1r.at[o],
            device_id={"head": other},
            device_id_type=MESH,
        )

    for o in range(1, n):
        w1copy(o).start()

    def project(j, first):
        x = xg[j].reshape(rows, feats)
        at = pl.ds(pl.multiple_of(j * feats, feats), feats)
        part = jnp.dot(x, w[at, :], preferred_element_type=F32)
        g = jnp.broadcast_to(gate[:, at].astype(F32), (size, feats)).astype(BF16)
        gpart = lax.dot_general(x, g, NT, preferred_element_type=F32)
        if first:
            pacc[...] = part
            gacc[...] = gpart
        else:
            pacc[...] += part
            gacc[...] += gpart

    loads[1].wait()
    loads[2].wait()
    project(me, True)
    loads[3].wait()
    for s in range(seqs):
        hi, lo = split(a32[s])
        a2[s, :size, :] = hi
        a2[s, size:, :] = lo
    loads[4].wait()

    def prepare(start, stop):
        for s in range(start, stop):
            hi, lo = split(m32[s].T)
            m2[s, :size, :] = hi
            m2[s, size:, :] = lo

    for at, o in enumerate(order):
        xcopy(o).wait_recv()
        project(lax.rem(me + n - o, n), False)
        prepare(seqs * at // (n - 1), seqs * (at + 1) // (n - 1))

    p = pacc[...]
    f = 0.8 + 0.2 * jax.nn.sigmoid(gacc[...] + bias_ref[...])
    q = p[:, :size]
    k = p[:, size : 2 * size]
    v = p[:, 2 * size :]
    k = k * lax.rsqrt(rowsum(k * k) + 1e-06)
    q = q * lax.rsqrt(rowsum(q * q) + 1e-06)
    kbuf[...] = k
    qbuf[...] = q
    for s in range(seqs):
        at = pl.ds(s, steps, stride=seqs)
        hi, lo = split(jnp.concatenate([kbuf[at, :], qbuf[at, :]], axis=0))
        left = jnp.concatenate(
            [jnp.concatenate([hi, hi], axis=1), jnp.concatenate([lo, lo], axis=1)], axis=0
        )
        r = jnp.dot(left, a2[s], preferred_element_type=F32)
        r = r[: 2 * steps] + r[2 * steps :]
        akbuf[at, :] = r[:steps]
        aqbuf[at, :] = r[steps:]

    def piece(x, t):
        return x[t * seqs : (t + 1) * seqs]

    ks = [piece(k, t) for t in range(steps)]
    qs_ = [piece(q, t) for t in range(steps)]
    vs = [piece(v, t) for t in range(steps)]
    fs = [piece(f, t) for t in range(steps)]
    ak = [akbuf[t * seqs : (t + 1) * seqs, :] for t in range(steps)]
    aq = [aqbuf[t * seqs : (t + 1) * seqs, :] for t in range(steps)]
    ws = []
    for t in range(steps):
        u = ak[t]
        rd = 1.0 / (fs[t] + rowsum(ks[t] * u))
        rf = 1.0 / fs[t]
        for i in range(t + 1, steps):
            ak[i] = (ak[i] - u * (rowsum(u * ks[i]) * rd)) * rf
        for i in range(t, steps):
            aq[i] = (aq[i] - u * (rowsum(u * qs_[i]) * rd)) * rf
        ws.append(aq[t])
        wbuf[t * seqs : (t + 1) * seqs, :] = aq[t]

    for s in range(seqs):
        at = pl.ds(s, steps, stride=seqs)
        hi, lo = split(wbuf[at, :])
        hi, lo = hi.astype(F32), lo.astype(F32)
        left = jnp.concatenate(
            [jnp.concatenate([hi, hi], axis=1), jnp.concatenate([lo, lo], axis=1)], axis=0
        ).astype(BF16)
        r = jnp.dot(left, m2[s], preferred_element_type=F32)
        robuf[at, :] = r[:steps] + r[steps:]

    decay = []
    whole = None
    pieces = []
    for t in range(steps):
        decay = [x * fs[t] for x in decay] + [None]
        whole = fs[t] if whole is None else whole * fs[t]
        total = whole * robuf[t * seqs : (t + 1) * seqs, :]
        for i in range(t + 1):
            e = rowsum(ks[i] * ws[t])
            total = total + (e * vs[i] if decay[i] is None else (e * decay[i]) * vs[i])
        decay[t] = jnp.ones_like(fs[t])
        pieces.append(total)
    ro = jnp.concatenate(pieces, axis=0)
    hi, lo = split(ro * ro)
    sqbuf[me] = lax.dot_general(
        jnp.ones((8, 2 * size), BF16),
        jnp.concatenate([hi, lo], axis=1),
        NT,
        preferred_element_type=F32,
    )
    rbuf[me] = (gain_ref[...] * ro).astype(BF16)

    def share(buf, send, recv, o):
        return pltpu.make_async_remote_copy(
            src_ref=buf.at[me],
            dst_ref=buf.at[me],
            send_sem=send.at[o],
            recv_sem=recv.at[o],
            device_id={"head": lax.rem(me + o, n)},
            device_id_type=MESH,
        )

    rcopy = functools.partial(share, rbuf, rs, rr)
    qcopy = functools.partial(share, sqbuf, qs, qr)
    for o in range(1, n):
        rcopy(o).start()
        qcopy(o).start()

    def w2copy(o, i):
        source = lax.rem(me + n - o, n)
        part = wout.at[source, pl.ds(pl.multiple_of(mine * slab, slab), slab)]
        return pltpu.make_async_remote_copy(
            src_ref=part,
            dst_ref=part,
            send_sem=w2s.at[o, i],
            recv_sem=w2r.at[o, i],
            device_id={"batch": base + lax.rem(mine + i, group)},
            device_id_type=MESH,
        )

    for o in range(1, n):
        w1copy(o).wait_recv()
        for i in range(1, group):
            w2copy(o, i).start()

    loads[5].wait()
    acc = jnp.dot(rbuf[me], wout[me], preferred_element_type=F32)
    squares = sqbuf[me]
    for o in range(1, n):
        source = lax.rem(me + n - o, n)
        rcopy(o).wait_recv()
        qcopy(o).wait_recv()
        for i in range(1, group):
            w2copy(o, i).wait_recv()
        acc = acc + jnp.dot(rbuf[source], wout[source], preferred_element_type=F32)
        squares = squares + sqbuf[source]
    scale = lax.rsqrt(squares[:1] / (n * size) + 1e-06)
    scale = jnp.broadcast_to(scale, (size, rows)).T
    for at in range(0, cols, size):
        out_ref[:, at : at + size] = acc[:, at : at + size] * scale

    for o in range(1, n):
        xcopy(o).wait_send()
        w1copy(o).wait_send()
        rcopy(o).wait_send()
        qcopy(o).wait_send()
        for i in range(1, group):
            w2copy(o, i).wait_send()


def local(n, batch, inputs, in_weight, gate_weight, gate_bias, norm_gain, out_weight, inv_gram, value_key):
    steps, seqs, feats = inputs.shape
    d_model, heads, width = in_weight.shape
    size = width // 3
    rows = steps * seqs
    cols = out_weight.shape[1] // n
    assert heads == 1
    group = math.gcd(math.gcd(batch, 8), out_weight.shape[0] // 16)
    anywhere = pl.BlockSpec(memory_space=pl.ANY)
    vmem = pl.BlockSpec(memory_space=pltpu.VMEM)
    dma = pltpu.SemaphoreType.DMA
    out = pl.pallas_call(
        functools.partial(kernel, n, group),
        out_shape=jax.ShapeDtypeStruct((rows, cols), F32),
        in_specs=[
            anywhere,
            anywhere,
            anywhere,
            vmem,
            vmem,
            anywhere,
            anywhere,
            anywhere,
        ],
        out_specs=vmem,
        scratch_shapes=[
            pltpu.VMEM((n, steps, seqs, feats), BF16),
            pltpu.VMEM((d_model, width), BF16),
            pltpu.VMEM((1, d_model), BF16),
            pltpu.VMEM((seqs, size, size), F32),
            pltpu.VMEM((seqs, size, size), F32),
            pltpu.VMEM((seqs, 2 * size, size), BF16),
            pltpu.VMEM((seqs, 2 * size, size), BF16),
            pltpu.VMEM((n, out_weight.shape[0], cols), BF16),
            pltpu.VMEM((rows, width), F32),
            pltpu.VMEM((rows, size), F32),
            pltpu.VMEM((rows, size), F32),
            pltpu.VMEM((rows, size), F32),
            pltpu.VMEM((rows, size), F32),
            pltpu.VMEM((rows, size), F32),
            pltpu.VMEM((rows, size), F32),
            pltpu.VMEM((rows, size), F32),
            pltpu.VMEM((n, rows, size), BF16),
            pltpu.VMEM((n, 8, rows), F32),
            dma((6,)),
            dma((n,)),
            dma((n,)),
            dma((n,)),
            dma((n,)),
            dma((n, group)),
            dma((n, group)),
            dma((n,)),
            dma((n,)),
            dma((n,)),
            dma((n,)),
        ],
        compiler_params=pltpu.CompilerParams(collective_id=0, has_side_effects=True),
    )(
        inputs,
        in_weight.reshape(d_model, width),
        gate_weight.reshape(1, d_model),
        gate_bias.reshape(1, 1),
        norm_gain.reshape(1, size),
        out_weight,
        inv_gram.reshape(seqs, size, size),
        value_key.reshape(seqs, size, size),
    )
    return out.reshape(steps, seqs, cols)


def solution(mesh):
    in_specs = (
        P(None, "batch", "head"),
        P(None, "head", None),
        P(None, "head"),
        P("head"),
        P("head"),
        P("head", None),
        P("batch", "head", None, None),
        P("batch", "head", None, None),
    )
    out_specs = P(None, "batch", "head")
    return jax.shard_map(
        functools.partial(local, mesh.shape["head"], mesh.shape["batch"]),
        mesh=mesh,
        in_specs=in_specs,
        out_specs=out_specs,
        check_vma=False,
    )
```

profile of v0, /device:TPU:0, one launch (start us, length us, event | category | flops | bytes accessed | tf_op | source)
XLA Modules:
  0.0 29.7 jit_solution(8241341821692485220)
XLA Ops:
  0.7 27.4 %shard_map.82 = f32[128,512]{1,0:T(8,128)} custom-call(bf16[8,16,512]{2,1,0:T(8,128)(2,1)} %x_hbm.1, bf16[2048,384]{1,0:T(8,128)(2,1)} %bitcast.8, bf16[1,2048]{1,0:T(2,128)(2,1)} %bitcast.12, f32[1,1]{1,0:T(1,128)} %bitcast.7.bias_ref, f32[1,128]{1,0:T(1,128)} %bitcast.13, bf16[128,2048]{1,0:T(8,128)(2,1)} %ow_hbm.1, f32[16,128,128]{2,1,0:T(8,128)} %bitcast.9, ...), custom_call_target="tpu_custom_call" | custom-call | tf_op jit(solution)/shard_map/pallas_call | solution.py:313
  28.0 1.7 %copy.11 = f32[8,16,512]{2,1,0:T(8,128)} copy(f32[8,16,512]{2,1,0:T(8,128)} %bitcast.11) | data formatting | bytes 524288
where the time goes:
time: 29.9 us; the launch traced here: 29.7 us
  Pallas kernels  27.4 us (92%)
  local copies, waits for them, and re-layouts  1.67 us (6%)
  between operations  0.66 us (2%)
    pallas_call x1, Pallas kernels, local(): pl.pallas_call(functools.partial(kernel, n, group), out_shape=jax.ShapeDt...  27.4 us
    unnamed x1, local copies, waits for them, and re-layouts  1.67 us

commit v1 on v0

v1 whole, which is shorter than its diff:
```python
import functools
import math

import jax
import jax.numpy as jnp
from jax import lax
from jax.experimental import pallas as pl
from jax.experimental.pallas import tpu as pltpu
from jax.sharding import PartitionSpec as P

MESH = pl.DeviceIdType.MESH
F32 = jnp.float32
BF16 = jnp.bfloat16
NT = (((1,), (1,)), ((), ()))
PIECES = 4
GROUPS = ((0, 1), (2, 3))


def split(x):
    hi = x.astype(BF16)
    lo = (x - hi.astype(F32)).astype(BF16)
    return hi, lo


def rowsum(x):
    return jnp.sum(x, axis=-1, keepdims=True)


def select(me, values):
    out = jnp.int32(values[0])
    for m in range(1, len(values)):
        out = jnp.where(me == m, jnp.int32(values[m]), out)
    return out


def arrivals(n, groups, width):
    out = []
    for m in range(n):
        found = []
        for j in range(n):
            for g in range(groups):
                hops = abs(j - m)
                late = 3.0 if j > m else 0.0
                found.append(((hops - 1) * groups * width + (g + 1) * width + 2.4 * hops + late, j, g))
        out.append([(j, g) for _, j, g in sorted(found) if j != m])
    return out


def kernel(
    n,
    group,
    x_hbm,
    w_hbm,
    gate_hbm,
    bias_hbm,
    gain_hbm,
    ow_hbm,
    a_hbm,
    m_hbm,
    out_ref,
    bias_ref,
    gain_ref,
    xg,
    w,
    gate,
    a32,
    m32,
    ab,
    wout,
    pacc,
    gacc,
    kq,
    abuf,
    bbuf,
    rbuf,
    sqbuf,
    lsem,
    xr,
    know,
    w1r,
    chip_r,
    core_r,
    early_r,
    rr,
    sent,
):
    steps, seqs, feats = x_hbm.shape
    rows = steps * seqs
    heads_rows = ow_hbm.shape[0]
    cols = ow_hbm.shape[1] // n
    size = a_hbm.shape[1]
    me = lax.axis_index("head")
    b = lax.axis_index("batch")
    mine = lax.rem(b, group)
    base = b - mine
    slab = heads_rows // group
    has_left = me > 0
    has_right = me < n - 1

    parity = lax.rem(mine, 2)
    chip = lax.div(mine, 2)
    chips = group // 2
    bits = chips.bit_length() - 1

    def flip(value, bit):
        return value + (1 - 2 * lax.rem(lax.div(value, 1 << bit), 2)) * (1 << bit)

    core_peer = base + mine + 1 - 2 * parity
    near = [base + 2 * flip(chip, bit) + parity for bit in range(bits)]
    place = parity * chips + chip

    barrier = pltpu.get_barrier_semaphore()

    @pl.when(has_left)
    def _():
        pl.semaphore_signal(barrier, inc=1, device_id={"head": me - 1}, device_id_type=MESH)

    @pl.when(has_right)
    def _():
        pl.semaphore_signal(barrier, inc=1, device_id={"head": me + 1}, device_id_type=MESH)

    for peer in [core_peer] + near:
        pl.semaphore_signal(barrier, inc=1, device_id={"batch": peer}, device_id_type=MESH)

    loads = [
        pltpu.make_async_copy(x_hbm, xg.at[me], lsem.at[0]),
        pltpu.make_async_copy(w_hbm, w, lsem.at[1]),
        pltpu.make_async_copy(gate_hbm, gate, lsem.at[1]),
        pltpu.make_async_copy(a_hbm, a32, lsem.at[1]),
        pltpu.make_async_copy(m_hbm, m32, lsem.at[1]),
        pltpu.make_async_copy(
            ow_hbm.at[:, pl.ds(pl.multiple_of(me * cols, cols), cols)], wout.at[me], lsem.at[1]
        ),
        pltpu.make_async_copy(bias_hbm, bias_ref, lsem.at[1]),
        pltpu.make_async_copy(gain_hbm, gain_ref, lsem.at[1]),
    ]
    for load in loads:
        load.start()

    order = [sorted((j for j in range(n) if j != m), key=lambda j: (abs(j - m), j)) for m in range(n)]
    sources = [select(me, [order[m][k] for m in range(n)]) for k in range(n - 1)]
    span = steps // PIECES

    groups = len(GROUPS)
    width = len(GROUPS[0])
    slots = arrivals(n, groups, width)
    slot_block = [select(me, [slots[m][k][0] for m in range(n)]) for k in range(len(slots[0]))]
    slot_group = [select(me, [slots[m][k][1] for m in range(n)]) for k in range(len(slots[0]))]
    early = max(k + 1 for m in range(n) for k, (_, g) in enumerate(slots[m]) if g == 0)

    def slot_of(j, receiver):
        return j - (j > receiver).astype(jnp.int32)

    def xcopy(side, j, c):
        part = xg.at[j, pl.ds(c * span, span)]
        peer = me + 2 * side - 1
        return pltpu.make_async_remote_copy(
            src_ref=part,
            dst_ref=part,
            send_sem=sent,
            recv_sem=xr.at[slot_of(j, peer), c],
            device_id={"head": peer},
            device_id_type=MESH,
        )

    def landed(part, sem):
        pltpu.make_async_remote_copy(
            src_ref=part,
            dst_ref=part,
            send_sem=sent,
            recv_sem=sem,
            device_id={"head": me},
            device_id_type=MESH,
        ).wait_recv()

    loads[0].wait()
    with jax.named_scope("barrier"):
        pl.semaphore_wait(barrier, has_left.astype(jnp.int32) + has_right.astype(jnp.int32) + 1 + bits)

    @pl.when(has_right)
    def _():
        for c in GROUPS[0]:
            xcopy(1, me, c).start()

    def send_rest():
        for c in range(width, PIECES):
            xcopy(1, me, c).start()

    @pl.when(has_right & (parity == 0))
    def _():
        send_rest()

    @pl.when(has_left)
    def _():
        for c in range(PIECES):
            xcopy(0, me, c).start()

    with jax.named_scope("know"):
        for d in range(2, n):

            @pl.when((me >= d - 1) & has_right)
            def _():
                pl.semaphore_signal(know.at[0], inc=1, device_id={"head": me + 1}, device_id_type=MESH)

            @pl.when(me >= d)
            def _():
                pl.semaphore_wait(know.at[0], 1)

        if bits == 2:
            pl.semaphore_signal(know.at[2], inc=1, device_id={"batch": near[0]}, device_id_type=MESH)

    def tell_left(d):
        @pl.when((me + d - 1 < n) & has_left)
        def _():
            pl.semaphore_signal(know.at[1], inc=1, device_id={"head": me - 1}, device_id_type=MESH)

    def hear_right(d):
        @pl.when(me + d < n)
        def _():
            pl.semaphore_wait(know.at[1], 1)

    if n > 2:
        tell_left(2)

    def w1copy(j):
        at = pl.ds(pl.multiple_of(place * slab, slab), slab)
        return pltpu.make_async_remote_copy(
            src_ref=ow_hbm.at[at, pl.ds(pl.multiple_of(j * cols, cols), cols)],
            dst_ref=wout.at[me, at],
            send_sem=sent,
            recv_sem=w1r,
            device_id={"head": j},
            device_id_type=MESH,
        )

    def w2copy(j, peer, sem, rows_sent, begin):
        part = wout.at[j, pl.ds(pl.multiple_of(begin, slab), rows_sent)]
        return pltpu.make_async_remote_copy(
            src_ref=part,
            dst_ref=part,
            send_sem=sent,
            recv_sem=sem,
            device_id={"batch": peer},
            device_id_type=MESH,
        )

    def chip_copies(j):
        return [
            w2copy(j, base + 2 * lax.rem(chip + o, chips) + parity, chip_r, slab, place * slab)
            for o in range(1, chips)
        ]

    def core_copy(j):
        return w2copy(j, core_peer, core_r, chips * slab, parity * chips * slab)

    def spread_chips():
        if bits == 2:
            pl.semaphore_wait(know.at[2], 1)
        landed(wout.at[: n - 1, :slab], w1r)
        for j in sources:
            for copy in chip_copies(j):
                copy.start()

    def spread_cores():
        landed(wout.at[: n - 1, : (chips - 1) * slab], chip_r)
        for j in sources:
            core_copy(j).start()

    def project(j, begin, count, first):
        x = xg[j, pl.ds(begin, count)].reshape(count * seqs, feats)
        at = pl.ds(pl.multiple_of(j * feats, feats), feats)
        part = jnp.dot(x, w[at, :], preferred_element_type=F32)
        g = jnp.broadcast_to(gate[:, at].astype(F32), (size, feats)).astype(BF16)
        gpart = lax.dot_general(x, g, NT, preferred_element_type=F32)
        at = pl.ds(pl.multiple_of(begin * seqs, seqs), count * seqs)
        if first:
            pacc[at, :] = part
            gacc[at, :] = gpart
        else:
            pacc[at, :] += part
            gacc[at, :] += gpart

    def prepare(start, stop):
        for s in range(start, stop):
            ah, al = split(a32[s])
            mh, ml = split(m32[s])
            bt = lax.dot_general(
                jnp.concatenate([ah, al], axis=1),
                jnp.concatenate([mh, mh], axis=1),
                NT,
                preferred_element_type=F32,
            )
            bt = bt + lax.dot_general(ah, ml, NT, preferred_element_type=F32)
            bh, bl = split(bt)
            ab[s, :size, :size] = ah
            ab[s, size:, :size] = al
            ab[s, :size, size:] = bh
            ab[s, size:, size:] = bl

    for j in sources:

        @pl.when(j < me)
        def _():
            w1copy(j).start()

    with jax.named_scope("proj0"):
        for load in loads[1:]:
            load.wait()
        project(me, 0, steps, True)
    with jax.named_scope("prepA"):
        prepare(0, seqs // 2)

    @pl.when(has_right & (parity == 1))
    def _():
        send_rest()

    @pl.when(me + 1 < n - 1)
    def _():
        w1copy(me + 1).start()

    def collect(begin, end):
        for k in range(begin, end):
            j, g = slot_block[k], slot_group[k]
            for at in range(width):
                c = g * width + at
                with jax.named_scope("x%d_%d" % (k, at)):
                    landed(xg.at[j, pl.ds(c * span, span)], xr.at[slot_of(j, me), c])

                @pl.when((j < me) & has_right)
                def _():
                    xcopy(1, j, c).start()

                @pl.when((j > me) & has_left)
                def _():
                    xcopy(0, j, c).start()

            with jax.named_scope("p%d" % k):
                project(j, g * width * span, width * span, False)
            if k < early:
                half = seqs // 2
                prepare(half + half * k // early, half + half * (k + 1) // early)

    past = []
    product = [None]

    def outgoing(part, j, sem):
        return pltpu.make_async_remote_copy(
            src_ref=part,
            dst_ref=part,
            send_sem=sent,
            recv_sem=sem,
            device_id={"head": j},
            device_id_type=MESH,
        )

    def rcopies(j, g):
        sem = rr.at[slot_of(me, j)] if g == groups - 1 else early_r.at[g]
        begin, end = g * width * span * seqs, (g + 1) * width * span * seqs
        return [
            outgoing(rbuf.at[me, pl.ds(begin, end - begin)], j, sem),
            outgoing(sqbuf.at[g, me], j, sem),
        ]

    def advance(g):
        first, last = GROUPS[g][0] * span, (GROUPS[g][-1] + 1) * span
        count = last - first
        half = count * seqs
        at = slice(first * seqs, last * seqs)
        p = pacc[at, :]
        f = 0.8 + 0.2 * jax.nn.sigmoid(gacc[at, :] + bias_ref[...])
        q = p[:, :size]
        k = p[:, size : 2 * size]
        v = p[:, 2 * size :]
        k = k * lax.rsqrt(rowsum(k * k) + 1e-06)
        q = q * lax.rsqrt(rowsum(q * q) + 1e-06)
        kq[:half, :] = k
        kq[half : 2 * half, :] = q
        for s in range(seqs):
            at = pl.ds(s, 2 * count, stride=seqs)
            hi, lo = split(kq[at, :])
            left = jnp.concatenate([hi.astype(F32), lo.astype(F32)], axis=0).astype(BF16)
            r = jnp.dot(jnp.concatenate([left, left], axis=1), ab[s], preferred_element_type=F32)
            r = r[: 2 * count] + r[2 * count :]
            abuf[at, :] = r[:, :size]
            bbuf[at, :] = r[:, size:]

        def piece(x, t):
            return x[t * seqs : (t + 1) * seqs]

        kt = [piece(k, t) for t in range(count)]
        qt = [piece(q, t) for t in range(count)]
        a = [u for u, _, _, _ in past] + [piece(abuf, t) for t in range(count)]
        dots = [[rowsum(a[s] * kt[t]) for s in range(first + t + 1)] for t in range(count)]
        reads = [[rowsum(a[s] * qt[t]) for s in range(first + t + 1)] for t in range(count)]
        pieces = []
        for t in range(count):
            ft = piece(f, t)
            product[0] = ft if product[0] is None else product[0] * ft
            now = first + t
            for s in range(now + 1):
                lower = past[s][1] if s < now else [past[r][2] * dots[t][r] for r in range(now)]
                for r in range(s):
                    dots[t][s] = dots[t][s] - lower[r] * dots[t][r]
                    reads[t][s] = reads[t][s] - lower[r] * reads[t][r]
            weight = 1.0 / (product[0] + dots[t][now])
            value = piece(v, t) - piece(bbuf, t)
            for s in range(now):
                value = value - dots[t][s] * past[s][3]
            past.append((a[now], [past[r][2] * dots[t][r] for r in range(now)], weight, weight * value))
            total = piece(bbuf, count + t)
            for s in range(now + 1):
                total = total + reads[t][s] * past[s][3]
            pieces.append(total)
        ro = jnp.concatenate(pieces, axis=0)
        hi, lo = split(ro * ro)
        both = jnp.concatenate([hi, lo], axis=1)
        sqbuf[g, me] = lax.dot_general(
            jnp.ones((8, 2 * size), BF16),
            jnp.concatenate([both] * (rows // half), axis=0),
            NT,
            preferred_element_type=F32,
        )
        rbuf[me, first * seqs : last * seqs] = (gain_ref[...] * ro).astype(BF16)
        for j in reversed(sources):
            for copy in rcopies(j, g):
                copy.start()

    inner = has_left & has_right
    collect(0, 1)
    if n > 2:
        hear_right(2)
        if n > 3:
            tell_left(3)
    collect(1, 2)
    with jax.named_scope("learn"):
        for d in range(3, n):
            hear_right(d)
            if d + 1 < n:
                tell_left(d + 1)

    for j in sources:

        @pl.when((j > me + 1) & ((j < n - 1) | (me == 0)))
        def _():
            w1copy(j).start()

    collect(2, early - 1)
    with jax.named_scope("spreadA0"):

        @pl.when(me == 0)
        def _():
            spread_chips()

    @pl.when(inner & (me < n - 2))
    def _():
        w1copy(n - 1).start()

    collect(early - 1, early)

    @pl.when(inner)
    def _():
        collect(early, len(slot_block))

    @pl.when((me == n - 2) | ((me == 0) & (n == 2)))
    def _():
        w1copy(n - 1).start()

    with jax.named_scope("spreadA1"):

        @pl.when(inner)
        def _():
            spread_chips()

    with jax.named_scope("adv0"):
        advance(0)

    @pl.when(jnp.logical_not(inner))
    def _():
        collect(early, len(slot_block))

    @pl.when(me == n - 1)
    def _():
        spread_chips()

    with jax.named_scope("adv1"):
        advance(1)

    with jax.named_scope("spreadB"):
        spread_cores()

    def send_done(part):
        pltpu.make_async_remote_copy(
            src_ref=part,
            dst_ref=part,
            send_sem=sent,
            recv_sem=w1r,
            device_id={"head": me},
            device_id_type=MESH,
        ).wait_send()

    with jax.named_scope("spreadC"):
        landed(wout.at[: n - 1, : chips * slab], core_r)

    def finish(g):
        part = slice(g * width * span * seqs, (g + 1) * width * span * seqs)
        count = width * span * seqs
        acc = jnp.dot(rbuf[me, part], wout[me], preferred_element_type=F32)
        squares = sqbuf[g, me]
        extra = 8 * rows * 4 // (size * 2)
        if g < groups - 1:
            landed(rbuf.at[: n - 1, : count + extra], early_r.at[g])
        for k, j in enumerate(sources):
            if g == groups - 1:
                with jax.named_scope("r%d" % k):
                    landed(rbuf.at[j, : count + extra], rr.at[slot_of(j, me)])
            acc = acc + jnp.dot(rbuf[j, part], wout[j], preferred_element_type=F32)
            squares = squares + sqbuf[g, j]
        scale = lax.rsqrt(squares[:1] / (n * size) + 1e-06)
        scale = jnp.broadcast_to(scale, (size, rows)).T[:count]
        for at in range(0, cols, size):
            out_ref[part, at : at + size] = acc[:, at : at + size] * scale

    for g in range(groups):
        if g == groups - 1:
            with jax.named_scope("sends"):
                @pl.when(has_right)
                def _():
                    send_done(xg.at[0])

                @pl.when(has_left)
                def _():
                    send_done(xg.at[0])

                for j in sources:

                    @pl.when(inner)
                    def _():
                        send_done(xg.at[0])

                for j in sources:
                    send_done(wout.at[0, :slab])
                    send_done(wout.at[0, : (chips - 1) * slab])
                    send_done(wout.at[0, : chips * slab])
                    for copy in rcopies(j, 0):
                        copy.wait_send()
        with jax.named_scope("finish%d" % g):
            finish(g)

    for j in sources:
        for copy in rcopies(j, groups - 1):
            copy.wait_send()


def local(n, batch, inputs, in_weight, gate_weight, gate_bias, norm_gain, out_weight, inv_gram, value_key):
    steps, seqs, feats = inputs.shape
    d_model, heads, width = in_weight.shape
    size = width // 3
    rows = steps * seqs
    cols = out_weight.shape[1] // n
    group = math.gcd(math.gcd(batch, 8), out_weight.shape[0] // 16)
    assert heads == 1 and steps % PIECES == 0 and group > 1
    anywhere = pl.BlockSpec(memory_space=pl.ANY)
    vmem = pl.BlockSpec(memory_space=pltpu.VMEM)
    dma = pltpu.SemaphoreType.DMA
    out = pl.pallas_call(
        functools.partial(kernel, n, group),
        out_shape=pltpu.VMEM((rows, cols), F32),
        in_specs=[anywhere] * 8,
        out_specs=vmem,
        scratch_shapes=[
            pltpu.VMEM((1, 1), F32),
            pltpu.VMEM((1, size), F32),
            pltpu.VMEM((n, steps, seqs, feats), BF16),
            pltpu.VMEM((d_model, width), BF16),
            pltpu.VMEM((1, d_model), BF16),
            pltpu.VMEM((seqs, size, size), F32),
            pltpu.VMEM((seqs, size, size), F32),
            pltpu.VMEM((seqs, 2 * size, 2 * size), BF16),
            pltpu.VMEM((n, out_weight.shape[0], cols), BF16),
            pltpu.VMEM((rows, width), F32),
            pltpu.VMEM((rows, size), F32),
            pltpu.VMEM((2 * rows, size), F32),
            pltpu.VMEM((2 * rows, size), F32),
            pltpu.VMEM((2 * rows, size), F32),
            pltpu.VMEM((n, rows, size), BF16),
            pltpu.VMEM((len(GROUPS), n, 8, rows), F32),
            dma((2,)),
            dma((n - 1, PIECES)),
            pltpu.SemaphoreType.REGULAR((3,)),
            dma,
            dma,
            dma,
            dma((len(GROUPS) - 1,)),
            dma((n - 1,)),
            dma,
        ],
        compiler_params=pltpu.CompilerParams(collective_id=0, has_side_effects=True),
    )(
        inputs,
        in_weight.reshape(d_model, width),
        gate_weight.reshape(1, d_model),
        gate_bias.reshape(1, 1),
        norm_gain.reshape(1, size),
        out_weight,
        inv_gram.reshape(seqs, size, size),
        value_key.reshape(seqs, size, size),
    )
    return out.reshape(steps, seqs, cols)


def solution(mesh):
    in_specs = (
        P(None, "batch", "head"),
        P(None, "head", None),
        P(None, "head"),
        P("head"),
        P("head"),
        P("head", None),
        P("batch", "head", None, None),
        P("batch", "head", None, None),
    )
    out_specs = P(None, "batch", "head")
    return jax.shard_map(
        functools.partial(local, mesh.shape["head"], mesh.shape["batch"]),
        mesh=mesh,
        in_specs=in_specs,
        out_specs=out_specs,
        check_vma=False,
    )
```

time: 29.9 us -> 22.5 us (0.75)
  Pallas kernels: 27.4 us -> 21 us
  local copies, waits for them, and re-layouts: 1.67 us -> 0.71 us
    pallas_call x1, Pallas kernels: 27.4 us -> 21 us  [local(): pl.pallas_call(functools.partial(kernel, n, group), out_shape=pltpu.VMEM(...]
    unnamed x1, local copies, waits for them, and re-layouts: 1.67 us -> 0.71 us
where the time goes in v1:
time: 22.5 us; the launch traced here: 22.4 us
  Pallas kernels  21 us (93%)
  local copies, waits for them, and re-layouts  0.71 us (3%)
  between operations  0.66 us (3%)
    pallas_call x1, Pallas kernels, local(): pl.pallas_call(functools.partial(kernel, n, group), out_shape=pltpu.VMEM(...  21 us
    unnamed x1, local copies, waits for them, and re-layouts  0.71 us

profile of v1, /device:TPU:0, one launch (start us, length us, event | category | flops | bytes accessed | tf_op | source)
XLA Modules:
  0.0 22.4 jit_solution(13609883355869580443)
XLA Ops:
  0.7 21.0 %shard_map.82 = f32[128,512]{1,0:T(8,128)S(1)} custom-call(bf16[8,16,512]{2,1,0:T(8,128)(2,1)} %x_hbm.1, bf16[2048,384]{1,0:T(8,128)(2,1)} %bitcast.9, bf16[1,2048]{1,0:T(2,128)(2,1)} %bitcast.12, f32[1,1]{1,0:T(1,128)} %bitcast.7.bias_hbm, f32[1,128]{1,0:T(1,128)} %bitcast.13, bf16[128,2048]{1,0:T(8,128)(2,1)} %ow_hbm.1, f32[16,128,128]{2,1,0:T(8,128)} %bitcast.10, ...), custom_call_target="tpu_custom_call" | custom-call | tf_op jit(solution)/shard_map/pallas_call | solution.py:565
  21.6 0.7 %copy.10 = f32[8,16,512]{2,1,0:T(8,128)} copy(f32[8,16,512]{2,1,0:T(8,128)S(1)} %bitcast.8) | data formatting | bytes 524288

commit v2 on v1

--- a/solution.py
+++ b/solution.py
@@ -40,7 +40,7 @@
         for j in range(n):
             for g in range(groups):
                 hops = abs(j - m)
-                late = 3.0 if j > m else 0.0
+                late = 0.0 if j < m else 1.7 if j == n - 1 and hops == 1 else 3.0
                 found.append(((hops - 1) * groups * width + (g + 1) * width + 2.4 * hops + late, j, g))
         out.append([(j, g) for _, j, g in sorted(found) if j != m])
     return out
@@ -77,6 +77,7 @@
     lsem,
     xr,
     know,
+    turn,
     w1r,
     chip_r,
     core_r,
@@ -93,7 +94,6 @@
     b = lax.axis_index("batch")
     mine = lax.rem(b, group)
     base = b - mine
-    slab = heads_rows // group
     has_left = me > 0
     has_right = me < n - 1
 
@@ -107,7 +107,8 @@
 
     core_peer = base + mine + 1 - 2 * parity
     near = [base + 2 * flip(chip, bit) + parity for bit in range(bits)]
-    place = parity * chips + chip
+    slab = heads_rows // chips
+    spreads = parity == 1
 
     barrier = pltpu.get_barrier_semaphore()
 
@@ -119,8 +120,12 @@
     def _():
         pl.semaphore_signal(barrier, inc=1, device_id={"head": me + 1}, device_id_type=MESH)
 
-    for peer in [core_peer] + near:
-        pl.semaphore_signal(barrier, inc=1, device_id={"batch": peer}, device_id_type=MESH)
+    pl.semaphore_signal(barrier, inc=1, device_id={"batch": core_peer}, device_id_type=MESH)
+
+    @pl.when(spreads)
+    def _():
+        for peer in near:
+            pl.semaphore_signal(barrier, inc=1, device_id={"batch": peer}, device_id_type=MESH)
 
     loads = [
         pltpu.make_async_copy(x_hbm, xg.at[me], lsem.at[0]),
@@ -175,7 +180,7 @@
 
     loads[0].wait()
     with jax.named_scope("barrier"):
-        pl.semaphore_wait(barrier, has_left.astype(jnp.int32) + has_right.astype(jnp.int32) + 1 + bits)
+        pl.semaphore_wait(barrier, has_left.astype(jnp.int32) + has_right.astype(jnp.int32) + 1 + bits * parity)
 
     @pl.when(has_right)
     def _():
@@ -186,7 +191,7 @@
         for c in range(width, PIECES):
             xcopy(1, me, c).start()
 
-    @pl.when(has_right & (parity == 0))
+    @pl.when(has_right)
     def _():
         send_rest()
 
@@ -207,7 +212,10 @@
                 pl.semaphore_wait(know.at[0], 1)
 
         if bits == 2:
-            pl.semaphore_signal(know.at[2], inc=1, device_id={"batch": near[0]}, device_id_type=MESH)
+
+            @pl.when(spreads)
+            def _():
+                pl.semaphore_signal(know.at[2], inc=1, device_id={"batch": near[0]}, device_id_type=MESH)
 
     def tell_left(d):
         @pl.when((me + d - 1 < n) & has_left)
@@ -223,7 +231,7 @@
         tell_left(2)
 
     def w1copy(j):
-        at = pl.ds(pl.multiple_of(place * slab, slab), slab)
+        at = pl.ds(pl.multiple_of(chip * slab, slab), slab)
         return pltpu.make_async_remote_copy(
             src_ref=ow_hbm.at[at, pl.ds(pl.multiple_of(j * cols, cols), cols)],
             dst_ref=wout.at[me, at],
@@ -244,34 +252,33 @@
             device_id_type=MESH,
         )
 
-    def chip_copies(j):
+    def chip_copies(k, j):
         return [
-            w2copy(j, base + 2 * lax.rem(chip + o, chips) + parity, chip_r, slab, place * slab)
+            w2copy(j, base + 2 * lax.rem(chip + o, chips) + parity, chip_r.at[k], slab, chip * slab)
             for o in range(1, chips)
         ]
 
-    def core_copy(j):
-        return w2copy(j, core_peer, core_r, chips * slab, parity * chips * slab)
+    def core_copy(k, j):
+        return w2copy(j, core_peer, core_r.at[k], heads_rows, 0)
 
     def spread_chips():
         if bits == 2:
             pl.semaphore_wait(know.at[2], 1)
         landed(wout.at[: n - 1, :slab], w1r)
-        for j in sources:
-            for copy in chip_copies(j):
+        for k, j in enumerate(sources):
+            for copy in chip_copies(k, j):
                 copy.start()
 
     def spread_cores():
-        landed(wout.at[: n - 1, : (chips - 1) * slab], chip_r)
-        for j in sources:
-            core_copy(j).start()
+        for k, j in enumerate(sources):
+            landed(wout.at[j, : (chips - 1) * slab], chip_r.at[k])
+            core_copy(k, j).start()
 
     def project(j, begin, count, first):
         x = xg[j, pl.ds(begin, count)].reshape(count * seqs, feats)
         at = pl.ds(pl.multiple_of(j * feats, feats), feats)
         part = jnp.dot(x, w[at, :], preferred_element_type=F32)
-        g = jnp.broadcast_to(gate[:, at].astype(F32), (size, feats)).astype(BF16)
-        gpart = lax.dot_general(x, g, NT, preferred_element_type=F32)
+        gpart = jnp.broadcast_to(rowsum(x.astype(F32) * gate[:, at].astype(F32)), (count * seqs, size))
         at = pl.ds(pl.multiple_of(begin * seqs, seqs), count * seqs)
         if first:
             pacc[at, :] = part
@@ -299,7 +306,7 @@
 
     for j in sources:
 
-        @pl.when(j < me)
+        @pl.when(spreads & (j < me))
         def _():
             w1copy(j).start()
 
@@ -308,25 +315,19 @@
             load.wait()
         project(me, 0, steps, True)
     with jax.named_scope("prepA"):
-        prepare(0, seqs // 2)
-
-    @pl.when(has_right & (parity == 1))
-    def _():
-        send_rest()
-
-    @pl.when(me + 1 < n - 1)
-    def _():
-        w1copy(me + 1).start()
+        prepare(0, seqs)
 
     def collect(begin, end):
         for k in range(begin, end):
             j, g = slot_block[k], slot_group[k]
+            far = has_right & (me - j >= 2)
+            held = far & (parity == 1) & (g == groups - 1)
             for at in range(width):
                 c = g * width + at
                 with jax.named_scope("x%d_%d" % (k, at)):
                     landed(xg.at[j, pl.ds(c * span, span)], xr.at[slot_of(j, me), c])
 
-                @pl.when((j < me) & has_right)
+                @pl.when((j < me) & has_right & jnp.logical_not(held))
                 def _():
                     xcopy(1, j, c).start()
 
@@ -334,11 +335,19 @@
                 def _():
                     xcopy(0, j, c).start()
 
+            @pl.when(far & (parity == 0) & (g == groups - 1))
+            def _():
+                pl.semaphore_signal(turn, inc=1, device_id={"batch": core_peer}, device_id_type=MESH)
+
+            @pl.when(held)
+            def _():
+                with jax.named_scope("t%d" % k):
+                    pl.semaphore_wait(turn, 1)
+                for c in GROUPS[-1]:
+                    xcopy(1, j, c).start()
+
             with jax.named_scope("p%d" % k):
                 project(j, g * width * span, width * span, False)
-            if k < early:
-                half = seqs // 2
-                prepare(half + half * k // early, half + half * (k + 1) // early)
 
     past = []
     product = [None]
@@ -360,6 +369,11 @@
             outgoing(rbuf.at[me, pl.ds(begin, end - begin)], j, sem),
             outgoing(sqbuf.at[g, me], j, sem),
         ]
+
+    def send_readouts(g):
+        for j in reversed(sources):
+            for copy in rcopies(j, g):
+                copy.start()
 
     def advance(g):
         first, last = GROUPS[g][0] * span, (GROUPS[g][-1] + 1) * span
@@ -419,11 +433,22 @@
             jnp.concatenate([both] * (rows // half), axis=0),
             NT,
             preferred_element_type=F32,
-        )
+        )[:1]
         rbuf[me, first * seqs : last * seqs] = (gain_ref[...] * ro).astype(BF16)
-        for j in reversed(sources):
-            for copy in rcopies(j, g):
-                copy.start()
+
+        if g < groups - 1:
+
+            @pl.when(jnp.logical_not(inner))
+            def _():
+                send_readouts(g)
+
+        else:
+            send_readouts(g)
+
+            @pl.when(inner)
+            def _():
+                for before in range(g):
+                    send_readouts(before)
 
     inner = has_left & has_right
     collect(0, 1)
@@ -438,55 +463,64 @@
             if d + 1 < n:
                 tell_left(d + 1)
 
+    collect(2, early - 2)
     for j in sources:
 
-        @pl.when((j > me + 1) & ((j < n - 1) | (me == 0)))
+        @pl.when(spreads & (me == 0) & (j < n - 1))
         def _():
             w1copy(j).start()
 
-    collect(2, early - 1)
-    with jax.named_scope("spreadA0"):
-
-        @pl.when(me == 0)
-        def _():
+    collect(early - 2, early - 1)
+
+    @pl.when(spreads & (me == 0))
+    def _():
+        w1copy(n - 1).start()
+        with jax.named_scope("spreadA0"):
             spread_chips()
 
-    @pl.when(inner & (me < n - 2))
-    def _():
-        w1copy(n - 1).start()
-
     collect(early - 1, early)
 
     @pl.when(inner)
     def _():
         collect(early, len(slot_block))
 
-    @pl.when((me == n - 2) | ((me == 0) & (n == 2)))
-    def _():
-        w1copy(n - 1).start()
-
-    with jax.named_scope("spreadA1"):
-
-        @pl.when(inner)
-        def _():
-            spread_chips()
+    for j in sources:
+
+        @pl.when(spreads & inner & (j > me) & (j < n - 1))
+        def _():
+            w1copy(j).start()
 
     with jax.named_scope("adv0"):
         advance(0)
 
+    @pl.when(spreads & inner)
+    def _():
+        w1copy(n - 1).start()
+
     @pl.when(jnp.logical_not(inner))
     def _():
         collect(early, len(slot_block))
 
-    @pl.when(me == n - 1)
-    def _():
-        spread_chips()
+    with jax.named_scope("spreadA1"):
+
+        @pl.when(spreads & (me == n - 1))
+        def _():
+            spread_chips()
 
     with jax.named_scope("adv1"):
         advance(1)
 
+    with jax.named_scope("spreadA"):
+
+        @pl.when(spreads & inner)
+        def _():
+            spread_chips()
+
     with jax.named_scope("spreadB"):
-        spread_cores()
+
+        @pl.when(spreads)
+        def _():
+            spread_cores()
 
     def send_done(part):
         pltpu.make_async_remote_copy(
@@ -498,24 +532,28 @@
             device_id_type=MESH,
         ).wait_send()
 
-    with jax.named_scope("spreadC"):
-        landed(wout.at[: n - 1, : chips * slab], core_r)
-
     def finish(g):
         part = slice(g * width * span * seqs, (g + 1) * width * span * seqs)
         count = width * span * seqs
         acc = jnp.dot(rbuf[me, part], wout[me], preferred_element_type=F32)
         squares = sqbuf[g, me]
-        extra = 8 * rows * 4 // (size * 2)
+        extra = rows * 4 // (size * 2)
         if g < groups - 1:
             landed(rbuf.at[: n - 1, : count + extra], early_r.at[g])
         for k, j in enumerate(sources):
+            if g == 0:
+
+                @pl.when(jnp.logical_not(spreads))
+                def _():
+                    with jax.named_scope("w%d" % k):
+                        landed(wout.at[j], core_r.at[k])
+
             if g == groups - 1:
                 with jax.named_scope("r%d" % k):
                     landed(rbuf.at[j, : count + extra], rr.at[slot_of(j, me)])
             acc = acc + jnp.dot(rbuf[j, part], wout[j], preferred_element_type=F32)
             squares = squares + sqbuf[g, j]
-        scale = lax.rsqrt(squares[:1] / (n * size) + 1e-06)
+        scale = lax.rsqrt(squares / (n * size) + 1e-06)
         scale = jnp.broadcast_to(scale, (size, rows)).T[:count]
         for at in range(0, cols, size):
             out_ref[part, at : at + size] = acc[:, at : at + size] * scale
@@ -538,13 +576,18 @@
                         send_done(xg.at[0])
 
                 for j in sources:
-                    send_done(wout.at[0, :slab])
-                    send_done(wout.at[0, : (chips - 1) * slab])
-                    send_done(wout.at[0, : chips * slab])
                     for copy in rcopies(j, 0):
                         copy.wait_send()
+
         with jax.named_scope("finish%d" % g):
             finish(g)
+
+    @pl.when(spreads)
+    def _():
+        for _ in sources:
+            send_done(wout.at[0, :slab])
+            send_done(wout.at[0, : (chips - 1) * slab])
+            send_done(wout.at[0])
 
     for j in sources:
         for copy in rcopies(j, groups - 1):
@@ -583,13 +626,14 @@
             pltpu.VMEM((2 * rows, size), F32),
             pltpu.VMEM((2 * rows, size), F32),
             pltpu.VMEM((n, rows, size), BF16),
-            pltpu.VMEM((len(GROUPS), n, 8, rows), F32),
+            pltpu.VMEM((len(GROUPS), n, 1, rows), F32),
             dma((2,)),
             dma((n - 1, PIECES)),
             pltpu.SemaphoreType.REGULAR((3,)),
+            pltpu.SemaphoreType.REGULAR,
             dma,
-            dma,
-            dma,
+            dma((n - 1,)),
+            dma((n - 1,)),
             dma((len(GROUPS) - 1,)),
             dma((n - 1,)),
             dma,

time: 22.5 us -> 21.2 us (0.942)
  Pallas kernels: 21 us -> 19.7 us
    pallas_call x1, Pallas kernels: 21 us -> 19.7 us  [local(): pl.pallas_call(functools.partial(kernel, n, group), out_shape=pltpu.VMEM(...]
where the time goes in v2:
time: 21.2 us; the launch traced here: 21.1 us
  Pallas kernels  19.7 us (93%)
  local copies, waits for them, and re-layouts  0.71 us (3%)
  between operations  0.66 us (3%)
    pallas_call x1, Pallas kernels, local(): pl.pallas_call(functools.partial(kernel, n, group), out_shape=pltpu.VMEM(...  19.7 us
    unnamed x1, local copies, waits for them, and re-layouts  0.71 us

profile of v2, /device:TPU:0, one launch (start us, length us, event | category | flops | bytes accessed | tf_op | source)
XLA Modules:
  0.0 21.1 jit_solution(2153107595544679650)
XLA Ops:
  0.7 19.7 %shard_map.82 = f32[128,512]{1,0:T(8,128)S(1)} custom-call(bf16[8,16,512]{2,1,0:T(8,128)(2,1)} %x_hbm.1, bf16[2048,384]{1,0:T(8,128)(2,1)} %bitcast.9, bf16[1,2048]{1,0:T(2,128)(2,1)} %bitcast.12, f32[1,1]{1,0:T(1,128)} %bitcast.7.bias_hbm, f32[1,128]{1,0:T(1,128)} %bitcast.13, bf16[128,2048]{1,0:T(8,128)(2,1)} %ow_hbm.1, f32[16,128,128]{2,1,0:T(8,128)} %bitcast.10, ...), custom_call_target="tpu_custom_call" | custom-call | tf_op jit(solution)/shard_map/pallas_call | solution.py:608
  20.4 0.7 %copy.10 = f32[8,16,512]{2,1,0:T(8,128)} copy(f32[8,16,512]{2,1,0:T(8,128)S(1)} %bitcast.8) | data formatting | bytes 524288
